TPU v7x, 32 devices: a whole 2x2x4 slice. The times are simulated.
32 devices in a mesh: view: 8 (over z, y), tok: 2 (over x), obj: 2 (over core).
Axes of the slice: x: 2, y: 2, z: 4, core: 2. Of those that a mesh axis runs over, the one named last changes fastest.
Arguments:
- latents: bfloat16 [512, 8, 2, 1280], P('tok', 'view', 'obj'), parts along dimension 2, may hold values from -8 to 8
- query_weight: bfloat16 [1280, 1024], P(None, 'tok'), may hold values from -2 to 2
- key_weight: bfloat16 [1280, 1024], P(None, 'tok'), may hold values from -14 to 14
- value_weight: bfloat16 [1280, 1024], P(None, 'tok'), may hold values from -0.15625 to 0.15625
- output_weight: bfloat16 [1024, 1280], P('tok'), may hold values from -0.1875 to 0.1875
- value_units: bfloat16 [1280, 5120], P(None, 'tok'), may hold values from -0.15625 to 0.15625
- gate_units: bfloat16 [1280, 5120], P(None, 'tok'), may hold values from -0.15625 to 0.15625
- down_weight: bfloat16 [5120, 1280], P('tok'), may hold values from -0.078125 to 0.078125
Outputs:
- refined: bfloat16 [512, 8, 2, 1280], P('tok', 'view', 'obj'), parts along dimension 2
There are 2 independent parts, one for each index of `obj`. A program takes and returns all parts, laid end to end along the dimension named above; an argument that names none is the same for every part. Nothing has to cross between parts.
All inputs are finite; a program needn't handle non-finite values.
Results may differ from a plain program's by a relative error of at most 0.012.
Values may be sent and summed in bfloat16 or wider, within the bound.
A program may use at most 128 MiB of HBM per device.

v0:
```python
import jax
import jax.numpy as jnp
from jax import lax
from jax.sharding import PartitionSpec as P

HS = 64


epsilon = 1e-05


def passed_along(block, axis, distance):
    devices = range(lax.axis_size(axis))
    route = [((i - distance) % len(devices), i) for i in devices]
    return lax.ppermute(block, axis, route)


def normalize(stream):
    average = jnp.mean(stream, -1, keepdims=True)
    centered = stream - average
    spread = jnp.mean(centered * centered, -1, keepdims=True)
    return centered * lax.rsqrt(spread + epsilon)


def on_device(
    latents,
    query_weight,
    key_weight,
    value_weight,
    output_weight,
    value_units,
    gate_units,
    down_weight,
):
    stream = latents.astype(jnp.float32)
    normed = normalize(stream).astype(jnp.bfloat16)
    joined = jnp.concatenate([query_weight, key_weight, value_weight], 1)
    projected = jnp.dot(
        lax.all_gather(normed, "tok", axis=0, tiled=True),
        joined,
        preferred_element_type=jnp.float32,
    ).astype(jnp.bfloat16)
    head_width = query_weight.shape[1]
    queries = projected[..., :head_width]
    key_part = projected[..., head_width : 2 * head_width]
    value_part = projected[..., 2 * head_width :]
    length_all, local_views, objects = (queries.shape[0], queries.shape[1], queries.shape[2])
    head_count = head_width // HS
    query_rows = length_all * local_views
    queries_flat = queries.reshape(query_rows, objects, head_count, HS)
    factor = HS ** (-0.5)

    def attend(states, key_block, value_block):
        key_rows = key_block.shape[0]

        def one_view(counter, inner):
            highest, totals, blended = inner
            key_view = lax.dynamic_index_in_dim(key_block, counter, 1, keepdims=False).reshape(
                key_rows, objects, head_count, HS
            )
            value_view = lax.dynamic_index_in_dim(value_block, counter, 1, keepdims=False).reshape(
                key_rows, objects, head_count, HS
            )
            scores = (
                jnp.einsum(
                    "ibhe,jbhe->bhij", queries_flat, key_view, preferred_element_type=jnp.float32
                )
                * factor
            )
            newest = jnp.maximum(highest, jnp.max(scores, -1))
            shrink = jnp.exp(highest - newest)
            weights = jnp.exp(scores - newest[..., None])
            totals = totals * shrink + jnp.sum(weights, -1)
            update = jnp.einsum(
                "bhij,jbhe->bhie",
                weights.astype(jnp.bfloat16),
                value_view,
                preferred_element_type=jnp.float32,
            )
            blended = blended * shrink[..., None] + update
            return (newest, totals, blended)

        return lax.fori_loop(0, key_block.shape[1], one_view, states)

    start_state = (
        jnp.full((objects, head_count, query_rows), -1e30, jnp.float32),
        jnp.zeros((objects, head_count, query_rows), jnp.float32),
        jnp.zeros((objects, head_count, query_rows, HS), jnp.float32),
    )
    stacked = jnp.stack([key_part, value_part])
    states = attend(start_state, key_part, value_part)

    def rotate(counter, bundle):
        inner, buffer_kv = bundle
        buffer_kv = passed_along(buffer_kv, "view", 1)
        return (attend(inner, buffer_kv[0], buffer_kv[1]), buffer_kv)

    states, stacked = lax.fori_loop(0, lax.axis_size("view") - 1, rotate, (states, stacked))
    highest, totals, blended = states
    attended = (blended / totals[..., None]).transpose(2, 0, 1, 3)
    attended = attended.reshape(length_all, local_views, objects, head_width).astype(jnp.bfloat16)
    full_output = lax.all_gather(output_weight, "tok", axis=0, tiled=True)
    own_rows = lax.all_to_all(attended, "tok", split_axis=0, concat_axis=3, tiled=True)
    groups = lax.axis_size("tok")
    grouped = own_rows.reshape(
        own_rows.shape[0], own_rows.shape[1], own_rows.shape[2], groups, head_width
    )
    weight_groups = full_output.reshape(groups, head_width, full_output.shape[1])
    group_parts = jnp.einsum(
        "rvbgc,gcd->rvbgd", grouped, weight_groups, preferred_element_type=jnp.float32
    ).astype(jnp.bfloat16)
    attention_out = jnp.sum(group_parts.astype(jnp.float32), 3)
    middle = stream + attention_out
    normed_two = normalize(middle).astype(jnp.bfloat16)
    gathered = lax.all_gather(normed_two, "tok", axis=0, tiled=True)
    linear = jnp.dot(gathered, value_units, preferred_element_type=jnp.float32)
    gating = jnp.dot(gathered, gate_units, preferred_element_type=jnp.float32)
    hidden = (linear * jax.nn.gelu(gating)).astype(jnp.bfloat16)
    feed_out = lax.psum_scatter(
        jnp.dot(hidden, down_weight, preferred_element_type=jnp.float32).astype(jnp.bfloat16),
        "tok",
        scatter_dimension=0,
        tiled=True,
    ).astype(jnp.float32)
    return (middle + feed_out).astype(jnp.bfloat16)


def solution(mesh):
    return jax.shard_map(
        on_device,
        mesh=mesh,
        in_specs=(
            P("tok", "view", "obj", None),
            P(None, "tok"),
            P(None, "tok"),
            P(None, "tok"),
            P("tok", None),
            P(None, "tok"),
            P(None, "tok"),
            P("tok", None),
        ),
        out_specs=P("tok", "view", "obj", None),
        check_vma=False,
    )
```

profile of v0, /device:TPU:0, one launch (start us, length us, event | category | flops | bytes accessed | tf_op | source)
XLA Modules:
  0.0 367.6 jit_solution(9363570284081747208)
XLA Ops:
  6.5 1.4 convert_reduce_fusion
  8.0 1.4 fusion.54
  9.4 2.3 fusion.55
  11.7 0.7 all-gather.6.cloned.1.call-update
  12.5 26.3 %all-gather.4.cloned.1.call-done = bf16[512,1,1,1280]{3,0,2,1:T(8,128)(2,1)} async-done(((bf16[256,1,1,1280]{3,0,2,1:T(8,128)(2,1)}), bf16[512,1,1,1280]{3,0,2,1:T(8,128)(2,1)}) %all-gather.4.cloned.1.call-update) | async-done | bytes 1310736 | tf_op jit(solution)/shard_map/all_gather | solution.py:39
  38.8 3.9 %fusion.42 = bf16[512,1,1,1536]{3,0,2,1:T(8,128)(2,1)S(1)} fusion(bf16[1280,512]{1,0:T(8,128)(2,1)S(1)} %copy-done.1, bf16[1280,512]{1,0:T(8,128)(2,1)S(1)} %copy-done.2, bf16[1280,512]{1,0:T(8,128)(2,1)} %param.11, bf16[512,1,1,1280]{3,0,2,1:T(8,128)(2,1)} %all-gather.4.cloned.1.call-done), kind=kOutput, calls=%fused_computation.44 | convolution fusion | flops 2025848832 | bytes 6815744 | tf_op jit(solution)/shard_map/dot_general | solution.py:38
  42.7 0.2 slice_bitcast_fusion.1
  43.1 0.2 copy.35
  43.3 4.9 %multiply_reduce_fusion.1 = (f32[8,512]{1,0:T(8,128)S(1)}, f32[8,512,512]{1,2,0:T(8,128)}) fusion(bf16[512,8,64]{0,2,1:T(8,128)(2,1)S(1)} %bitcast.98, bf16[512,8,64]{0,2,1:T(8,128)(2,1)S(1)} %bitcast.105), kind=kOutput, calls=%fused_computation.17 | convolution fusion | flops 272625664 | bytes 9453568 | tf_op jit(solution)/shard_map/while/body/eval_jaxpr/ibhe,jbhe->bhij/dot_general | solution.py:65
  48.3 0.2 copy.36
  48.5 5.2 %fusion.17 = f32[8,512]{1,0:T(8,128)S(1)} fusion(f32[8,512,512]{1,2,0:T(8,128)} %get-tuple-element.139, f32[8,512]{1,0:T(8,128)S(1)} %get-tuple-element.137), kind=kLoop, calls=%fused_computation.20 | loop fusion | flops 6287360 | bytes 8421376 | tf_op jit(solution)/shard_map/while/body/eval_jaxpr/reduce_sum | solution.py:73
  53.8 1.3 copy.39
  55.2 4.9 %fusion.51 = f32[1,8,512,64]{2,3,1,0:T(8,128)S(1)} fusion(bf16[512,8,64]{0,2,1:T(8,128)(2,1)S(1)} %bitcast.104, f32[8,512,512]{1,2,0:T(8,128)} %get-tuple-element.139, f32[8,512]{1,0:T(8,128)S(1)} %get-tuple-element.137, f32[8,512]{1,0:T(8,128)S(1)} %get-tuple-element.135), kind=kOutput, calls=%fused_computation.52 | convolution fusion | flops 274989056 | bytes 9994240 | tf_op jit(solution)/shard_map/while/body/eval_jaxpr/bhij,jbhe->bhie/dot_general | solution.py:74
  60.1 214.6 %while.2 = (s32[]{:T(128)}, f32[1,8,512]{2,1,0:T(8,128)S(1)}, f32[1,8,512]{2,1,0:T(8,128)S(1)}, f32[1,8,512,64]{2,3,1,0:T(8,128)S(1)}, bf16[2,512,1,1,512]{1,4,3...) while((s32[]{:T(128)}, f32[1,8,512]{2,1,0:T(8,128)S(1)}, f32[1,8,512]{2,1,0:T(8,128)S(1)}, ...), condition=%wide.region_7.8_spmd, body=%wide.region_4.7_spmd.sunk | while | flops 554184704 | bytes 37486708 | solution.py:98
  60.1 1.5 collective-permute-start
  61.6 26.1 %collective-permute-done = bf16[2,512,1,1,512]{1,4,3,2,0:T(8,128)(2,1)S(1)} collective-permute-done((bf16[2,512,1,1,512]{1,4,3,2,0:T(8,128)(2,1)}, bf16[2,512,1,1,512]{1,4,3,2,0:T(8,128)(2,1)S(1)}, u32[]{:S(2)}, u32[]{:S(2)}) %collective-permute-start) | collective-permute-done | bytes 1048608 | tf_op jit(solution)/shard_map/while/body/eval_jaxpr/ppermute | solution.py:15
  87.8 1.3 multiply_reduce_fusion.4
  89.2 1.4 fusion.93
  90.6 1.8 fusion.94
  92.4 1.0 copy.59
  93.4 26.7 %collective-permute-done = bf16[2,512,1,1,512]{1,4,3,2,0:T(8,128)(2,1)S(1)} collective-permute-done((bf16[2,512,1,1,512]{1,4,3,2,0:T(8,128)(2,1)}, bf16[2,512,1,1,512]{1,4,3,2,0:T(8,128)(2,1)S(1)}, u32[]{:S(2)}, u32[]{:S(2)}) %collective-permute-start) | collective-permute-done | bytes 1048608 | tf_op jit(solution)/shard_map/while/body/eval_jaxpr/ppermute | solution.py:15
  120.2 1.3 multiply_reduce_fusion.4
  121.5 1.4 fusion.93
  123.0 1.8 fusion.94
  124.8 1.0 copy.59
  125.8 25.9 %collective-permute-done = bf16[2,512,1,1,512]{1,4,3,2,0:T(8,128)(2,1)S(1)} collective-permute-done((bf16[2,512,1,1,512]{1,4,3,2,0:T(8,128)(2,1)}, bf16[2,512,1,1,512]{1,4,3,2,0:T(8,128)(2,1)S(1)}, u32[]{:S(2)}, u32[]{:S(2)}) %collective-permute-start) | collective-permute-done | bytes 1048608 | tf_op jit(solution)/shard_map/while/body/eval_jaxpr/ppermute | solution.py:15
  151.7 1.3 multiply_reduce_fusion.4
  153.0 1.4 fusion.93
  154.5 1.8 fusion.94
  156.3 1.0 copy.59
  157.3 25.0 %collective-permute-done = bf16[2,512,1,1,512]{1,4,3,2,0:T(8,128)(2,1)S(1)} collective-permute-done((bf16[2,512,1,1,512]{1,4,3,2,0:T(8,128)(2,1)}, bf16[2,512,1,1,512]{1,4,3,2,0:T(8,128)(2,1)S(1)}, u32[]{:S(2)}, u32[]{:S(2)}) %collective-permute-start) | collective-permute-done | bytes 1048608 | tf_op jit(solution)/shard_map/while/body/eval_jaxpr/ppermute | solution.py:15
  182.3 1.3 multiply_reduce_fusion.4
  183.7 1.4 fusion.93
  185.1 1.8 fusion.94
  186.9 1.0 copy.59
  187.9 24.1 %collective-permute-done = bf16[2,512,1,1,512]{1,4,3,2,0:T(8,128)(2,1)S(1)} collective-permute-done((bf16[2,512,1,1,512]{1,4,3,2,0:T(8,128)(2,1)}, bf16[2,512,1,1,512]{1,4,3,2,0:T(8,128)(2,1)S(1)}, u32[]{:S(2)}, u32[]{:S(2)}) %collective-permute-start) | collective-permute-done | bytes 1048608 | tf_op jit(solution)/shard_map/while/body/eval_jaxpr/ppermute | solution.py:15
  212.1 1.3 multiply_reduce_fusion.4
  213.5 1.4 fusion.93
  214.9 1.8 fusion.94
  216.7 1.0 copy.59
  217.7 23.3 %collective-permute-done = bf16[2,512,1,1,512]{1,4,3,2,0:T(8,128)(2,1)S(1)} collective-permute-done((bf16[2,512,1,1,512]{1,4,3,2,0:T(8,128)(2,1)}, bf16[2,512,1,1,512]{1,4,3,2,0:T(8,128)(2,1)S(1)}, u32[]{:S(2)}, u32[]{:S(2)}) %collective-permute-start) | collective-permute-done | bytes 1048608 | tf_op jit(solution)/shard_map/while/body/eval_jaxpr/ppermute | solution.py:15
  241.1 1.3 multiply_reduce_fusion.4
  242.4 1.4 fusion.93
  243.8 1.8 fusion.94
  245.6 1.0 copy.59
  246.6 22.4 %collective-permute-done = bf16[2,512,1,1,512]{1,4,3,2,0:T(8,128)(2,1)S(1)} collective-permute-done((bf16[2,512,1,1,512]{1,4,3,2,0:T(8,128)(2,1)}, bf16[2,512,1,1,512]{1,4,3,2,0:T(8,128)(2,1)S(1)}, u32[]{:S(2)}, u32[]{:S(2)}) %collective-permute-start) | collective-permute-done | bytes 1048608 | tf_op jit(solution)/shard_map/while/body/eval_jaxpr/ppermute | solution.py:15
  269.1 1.3 multiply_reduce_fusion.4
  270.5 1.4 fusion.93
  271.9 1.8 fusion.94
  273.7 1.0 copy.59
  274.8 0.5 broadcast.142
  275.3 1.0 reduce.16
  276.4 0.2 copy.44
  276.6 0.4 reshape.223
  277.0 9.6 %all_to_all.15 = bf16[2,2,65536]{2,1,0:T(2,128)(2,1)S(1)} all-to-all(bf16[2,2,65536]{2,1,0:T(2,128)(2,1)S(1)} %reshape.223), channel_id=1, replica_groups=mesh['view'=8,'tok'=2,'obj'=2] {'tok'}, dimensions={0} | all-to-all | bytes 1048576 | tf_op jit(solution)/shard_map/all_to_all | solution.py:103
  286.6 0.5 reshape.224
  287.2 2.7 fusion.45
  290.1 0.3 multiply_reduce_fusion.2
  290.5 1.1 multiply_convert_fusion
  291.6 20.2 %all-gather.8.cloned.1.call-done = bf16[512,1,1,1280]{3,0,2,1:T(8,128)(2,1)} async-done(((bf16[256,1,1,1280]{3,0,2,1:T(8,128)(2,1)}), bf16[512,1,1,1280]{3,0,2,1:T(8,128)(2,1)}) %all-gather.8.cloned.1.call-update) | async-done | bytes 1310736 | tf_op jit(solution)/shard_map/all_gather | solution.py:115
  311.8 9.2 %fusion.56 = f32[512,2560]{1,0:T(8,128)} fusion(bf16[1280,2560]{1,0:T(8,128)(2,1)} %param.16, bf16[512,1,1,1280]{3,0,2,1:T(8,128)(2,1)} %all-gather.8.cloned.1.call-done), kind=kOutput, calls=%fused_computation.55 | convolution fusion | flops 3355443200 | bytes 13107200 | tf_op jit(solution)/shard_map/dot_general | solution.py:117
  321.0 14.5 %fusion.41 = bf16[512,1,1,1280]{3,0,2,1:T(8,128)(2,1)} fusion(bf16[2560,1280]{1,0:T(8,128)(2,1)} %param.17, f32[512,2560]{1,0:T(8,128)} %fusion.56, bf16[1280,2560]{1,0:T(8,128)(2,1)} %param.15, bf16[512,1,1,1280]{3,0,2,1:T(8,128)(2,1)S(1)} %copy-done.3), kind=kOutput, calls=%fused_computation.43 | convolution fusion | flops 6724648960 | bytes 20971520 | tf_op jit(solution)/shard_map/dot_general | solution.py:120
  335.5 23.4 %reduce-scatter.2.cloned.1.call-done = bf16[256,1,1,1280]{3,0,2,1:T(8,128)(2,1)} async-done(((bf16[512,1,1,1280]{3,0,2,1:T(8,128)(2,1)}), bf16[256,1,1,1280]{3,0,2,1:T(8,128)(2,1)}) %reduce-scatter.2.cloned.1.call-update) | async-done | bytes 655376 | tf_op jit(solution)/shard_map/reduce_scatter | solution.py:119
  358.9 2.1 add_convert_fusion
  (61 shorter events, 1.7 us)
Async XLA Ops:
  6.5 32.2 %copy-start.2 = (bf16[1280,512]{1,0:T(8,128)(2,1)S(1)}, bf16[1280,512]{1,0:T(8,128)(2,1)}, u32[]{:S(2)}) copy-start(bf16[1280,512]{1,0:T(8,128)(2,1)} %param.12) | copy-start | bytes 3932164
  6.5 32.2 %copy-start.1 = (bf16[1280,512]{1,0:T(8,128)(2,1)S(1)}, bf16[1280,512]{1,0:T(8,128)(2,1)}, u32[]{:S(2)}) copy-start(bf16[1280,512]{1,0:T(8,128)(2,1)} %param.13) | copy-start | bytes 3932164
  6.5 32.2 %all-gather.4.cloned.1.call-start = ((), (), s32[]{:S(2)}) async-start(), calls=%async_computation.2 | async-start | bytes 1966080 | tf_op jit(solution)/shard_map/all_gather | solution.py:39
  11.7 275.6 %all-gather.6.cloned.1.call-start = ((), (), s32[]{:S(2)}) async-start(), calls=%async_computation.3 | async-start | bytes 3932160 | tf_op jit(solution)/shard_map/all_gather | solution.py:102
  12.4 299.4 %all-gather.8.cloned.1.call-start = ((), (), s32[]{:S(2)}) async-start(), calls=%async_computation.4 | async-start | bytes 1966080 | tf_op jit(solution)/shard_map/all_gather | solution.py:115
  60.1 27.6 %collective-permute-start = (bf16[2,512,1,1,512]{1,4,3,2,0:T(8,128)(2,1)}, bf16[2,512,1,1,512]{1,4,3,2,0:T(8,128)(2,1)S(1)}, u32[]{:S(2)}, u32[]{:S(2)}) collective-permute-start(bf16[2,512,1,1,512]{1,4,3,2,0:T(8,128)(2,1)} %get-tuple-element.200), channel_id=1, source_target_pairs={{28,0},{0,4},{4,8},{8,12},{12,16},{16,20},{20,24},{24,28},{29,1},{... | collective-permute-start | bytes 3145736 | tf_op jit(solution)/shard_map/while/body/eval_jaxpr/ppermute | solution.py:15
  93.4 26.7 %collective-permute-start = (bf16[2,512,1,1,512]{1,4,3,2,0:T(8,128)(2,1)}, bf16[2,512,1,1,512]{1,4,3,2,0:T(8,128)(2,1)S(1)}, u32[]{:S(2)}, u32[]{:S(2)}) collective-permute-start(bf16[2,512,1,1,512]{1,4,3,2,0:T(8,128)(2,1)} %get-tuple-element.200), channel_id=1, source_target_pairs={{28,0},{0,4},{4,8},{8,12},{12,16},{16,20},{20,24},{24,28},{29,1},{... | collective-permute-start | bytes 3145736 | tf_op jit(solution)/shard_map/while/body/eval_jaxpr/ppermute | solution.py:15
  125.8 25.9 %collective-permute-start = (bf16[2,512,1,1,512]{1,4,3,2,0:T(8,128)(2,1)}, bf16[2,512,1,1,512]{1,4,3,2,0:T(8,128)(2,1)S(1)}, u32[]{:S(2)}, u32[]{:S(2)}) collective-permute-start(bf16[2,512,1,1,512]{1,4,3,2,0:T(8,128)(2,1)} %get-tuple-element.200), channel_id=1, source_target_pairs={{28,0},{0,4},{4,8},{8,12},{12,16},{16,20},{20,24},{24,28},{29,1},{... | collective-permute-start | bytes 3145736 | tf_op jit(solution)/shard_map/while/body/eval_jaxpr/ppermute | solution.py:15
  157.3 25.0 %collective-permute-start = (bf16[2,512,1,1,512]{1,4,3,2,0:T(8,128)(2,1)}, bf16[2,512,1,1,512]{1,4,3,2,0:T(8,128)(2,1)S(1)}, u32[]{:S(2)}, u32[]{:S(2)}) collective-permute-start(bf16[2,512,1,1,512]{1,4,3,2,0:T(8,128)(2,1)} %get-tuple-element.200), channel_id=1, source_target_pairs={{28,0},{0,4},{4,8},{8,12},{12,16},{16,20},{20,24},{24,28},{29,1},{... | collective-permute-start | bytes 3145736 | tf_op jit(solution)/shard_map/while/body/eval_jaxpr/ppermute | solution.py:15
  187.9 24.2 %collective-permute-start = (bf16[2,512,1,1,512]{1,4,3,2,0:T(8,128)(2,1)}, bf16[2,512,1,1,512]{1,4,3,2,0:T(8,128)(2,1)S(1)}, u32[]{:S(2)}, u32[]{:S(2)}) collective-permute-start(bf16[2,512,1,1,512]{1,4,3,2,0:T(8,128)(2,1)} %get-tuple-element.200), channel_id=1, source_target_pairs={{28,0},{0,4},{4,8},{8,12},{12,16},{16,20},{20,24},{24,28},{29,1},{... | collective-permute-start | bytes 3145736 | tf_op jit(solution)/shard_map/while/body/eval_jaxpr/ppermute | solution.py:15
  217.7 23.3 %collective-permute-start = (bf16[2,512,1,1,512]{1,4,3,2,0:T(8,128)(2,1)}, bf16[2,512,1,1,512]{1,4,3,2,0:T(8,128)(2,1)S(1)}, u32[]{:S(2)}, u32[]{:S(2)}) collective-permute-start(bf16[2,512,1,1,512]{1,4,3,2,0:T(8,128)(2,1)} %get-tuple-element.200), channel_id=1, source_target_pairs={{28,0},{0,4},{4,8},{8,12},{12,16},{16,20},{20,24},{24,28},{29,1},{... | collective-permute-start | bytes 3145736 | tf_op jit(solution)/shard_map/while/body/eval_jaxpr/ppermute | solution.py:15
  246.6 22.4 %collective-permute-start = (bf16[2,512,1,1,512]{1,4,3,2,0:T(8,128)(2,1)}, bf16[2,512,1,1,512]{1,4,3,2,0:T(8,128)(2,1)S(1)}, u32[]{:S(2)}, u32[]{:S(2)}) collective-permute-start(bf16[2,512,1,1,512]{1,4,3,2,0:T(8,128)(2,1)} %get-tuple-element.200), channel_id=1, source_target_pairs={{28,0},{0,4},{4,8},{8,12},{12,16},{16,20},{20,24},{24,28},{29,1},{... | collective-permute-start | bytes 3145736 | tf_op jit(solution)/shard_map/while/body/eval_jaxpr/ppermute | solution.py:15
  286.6 3.3 copy-start
  291.6 67.4 %reduce-scatter.2.cloned.1.call-start = ((), (), s32[]{:S(2)}) async-start(), calls=%async_computation.5 | async-start | bytes 1966080 | tf_op jit(solution)/shard_map/reduce_scatter | solution.py:119
  311.8 9.2 %copy-start.3 = (bf16[512,1,1,1280]{3,0,2,1:T(8,128)(2,1)S(1)}, bf16[512,1,1,1280]{3,0,2,1:T(8,128)(2,1)}, u32[]{:S(2)}) copy-start(bf16[512,1,1,1280]{3,0,2,1:T(8,128)(2,1)} %all-gather.8.cloned.1.call-done) | copy-start | bytes 3932164
Sparse Core Ops, SparseCore 0:
  11.8 26.9 all-gather.3
  40.3 38.9 all-gather.5
  291.7 20.0 all-gather.7
  335.6 23.2 reduce-scatter.1
where the time goes:
time: 368 us
  waiting for transfers between devices  244 us (66%)
  matrix products  62 us (17%)
  other arithmetic  25.2 us (7%)
  between operations  13.3 us (4%)
  local copies, waits for them, and re-layouts  11.3 us (3%)
  blocking collectives  9.56 us (3%)
    ppermute x7, waiting for transfers between devices, passed_along(): return lax.ppermute(block, axis, route)  174 us
    all_gather x1, waiting for transfers between devices, on_device(): lax.all_gather(normed, 'tok', axis=0, tiled=True)  26.3 us
    reduce_scatter x1, waiting for transfers between devices, on_device(): lax.psum_scatter(jnp.dot(hidden, down_weight, preferred_element_type=jnp....  23.4 us
    all_gather x1, waiting for transfers between devices, on_device(): gathered = lax.all_gather(normed_two, 'tok', axis=0, tiled=True)  20.2 us
    dot_general x8, matrix products, one_view(): jnp.einsum('bhij,jbhe->bhie', weights.astype(jnp.bfloat16), value_view, p...  17.7 us
    reduce_sum x8, other arithmetic, one_view(): totals = totals * shrink + jnp.sum(weights, -1)  14.9 us
    dot_general x1, matrix products, on_device(): jnp.dot(hidden, down_weight, preferred_element_type=jnp.float32)  14.5 us
    dot_general x8, matrix products, one_view(): jnp.einsum('ibhe,jbhe->bhij', queries_flat, key_view, preferred_element_t...  14.1 us
  transfers between devices with their start and end apart: 11, of which 10 were waited for; matrix products, arithmetic and copies ran while one was open for 17% of the time, Pallas kernels for 0%

commit v1 on v0

--- a/solution.py
+++ b/solution.py
@@ -1,9 +1,16 @@
+import functools
+
 import jax
 import jax.numpy as jnp
 from jax import lax
+from jax.experimental import pallas as pl
+from jax.experimental.pallas import tpu as pltpu
 from jax.sharding import PartitionSpec as P
 
 HS = 64
+MESH = pl.DeviceIdType.MESH
+VMEM = pl.BlockSpec(memory_space=pltpu.VMEM)
+ANY = pl.BlockSpec(memory_space=pl.ANY)
 
 
 epsilon = 1e-05
@@ -22,7 +29,250 @@
     return centered * lax.rsqrt(spread + epsilon)
 
 
-def on_device(
+def meet(axes):
+    barrier = pltpu.get_barrier_semaphore()
+    for peer in axes:
+        pl.semaphore_signal(barrier, inc=1, device_id=peer, device_id_type=MESH)
+    pl.semaphore_wait(barrier, len(axes))
+
+
+def peers_of(axis, count):
+    me = lax.axis_index(axis)
+    return [lax.rem(me + d, count) for d in range(1, count)]
+
+
+def post(sources, results, axis, count, send_sem, recv_sem, own_sem, scattered):
+    me = lax.axis_index(axis)
+    waits = []
+    for number, (source, result) in enumerate(zip(sources, results)):
+        for d in range(1, count):
+            peer = lax.rem(me + d, count)
+            sender = lax.rem(me - d + count, count)
+            copy = pltpu.make_async_remote_copy(
+                src_ref=source.at[peer] if scattered else source,
+                dst_ref=result.at[me],
+                send_sem=send_sem.at[number, d],
+                recv_sem=recv_sem.at[number, d],
+                device_id={axis: peer},
+                device_id_type=MESH,
+            )
+            arrival = pltpu.make_async_remote_copy(
+                src_ref=source.at[peer] if scattered else source,
+                dst_ref=result.at[sender],
+                send_sem=send_sem.at[number, d],
+                recv_sem=recv_sem.at[number, d],
+                device_id={axis: peer},
+                device_id_type=MESH,
+            )
+            copy.start()
+            waits.append(copy.wait_send)
+            waits.append(arrival.wait_recv)
+        own = pltpu.make_async_copy(
+            source.at[me] if scattered else source, result.at[me], own_sem.at[number]
+        )
+        own.start()
+        waits.append(own.wait)
+    return waits
+
+
+def token_kernel(count, scattered, x_ref, out_ref, send_sem, recv_sem, own_sem):
+    meet([{"tok": p} for p in peers_of("tok", count)])
+    for wait in post([x_ref], [out_ref], "tok", count, send_sem, recv_sem, own_sem, scattered):
+        wait()
+
+
+def over_tokens(x, count, scattered, number):
+    block = x.shape[1:] if scattered else x.shape
+    return pl.pallas_call(
+        functools.partial(token_kernel, count, scattered),
+        out_shape=jax.ShapeDtypeStruct((count,) + block, x.dtype),
+        in_specs=[VMEM],
+        out_specs=ANY,
+        scratch_shapes=[
+            pltpu.SemaphoreType.DMA((1, count)),
+            pltpu.SemaphoreType.DMA((1, count)),
+            pltpu.SemaphoreType.DMA((1,)),
+        ],
+        compiler_params=pltpu.CompilerParams(collective_id=number, has_side_effects=True),
+        name=f"over_tokens_{number}",
+    )(x)
+
+
+def heads_kernel(views, toks, q, k, v, w, q_out, k_out, v_out, w_out, *sems):
+    meet(
+        [{"view": p} for p in peers_of("view", views)]
+        + [{"tok": p} for p in peers_of("tok", toks)]
+    )
+    waits = post([q, k, v], [q_out, k_out, v_out], "view", views, *sems[:3], True)
+    waits += post([w], [w_out], "tok", toks, *sems[3:], False)
+    for wait in waits:
+        wait()
+
+
+def spread_heads(queries, keys, values, weight, views, toks):
+    like = jax.ShapeDtypeStruct(queries.shape, queries.dtype)
+    return pl.pallas_call(
+        functools.partial(heads_kernel, views, toks),
+        out_shape=(like, like, like, jax.ShapeDtypeStruct((toks,) + weight.shape, weight.dtype)),
+        in_specs=[VMEM] * 4,
+        out_specs=(ANY,) * 4,
+        scratch_shapes=[
+            pltpu.SemaphoreType.DMA((3, views)),
+            pltpu.SemaphoreType.DMA((3, views)),
+            pltpu.SemaphoreType.DMA((3,)),
+            pltpu.SemaphoreType.DMA((1, toks)),
+            pltpu.SemaphoreType.DMA((1, toks)),
+            pltpu.SemaphoreType.DMA((1,)),
+        ],
+        compiler_params=pltpu.CompilerParams(collective_id=1, has_side_effects=True),
+        name="spread_heads",
+    )(queries, keys, values, weight)
+
+
+def attention_kernel(
+    views, toks, q_ref, k_ref, v_ref, out_ref, keys, staged, send_sem, recv_sem, own_sem
+):
+    view, tok = lax.axis_index("view"), lax.axis_index("tok")
+    others = [
+        (dv, dt) for dv in range(views) for dt in range(toks) if dv or dt
+    ]
+    meet(
+        [
+            {"view": lax.rem(view + dv, views), "tok": lax.rem(tok + dt, toks)}
+            for dv, dt in others
+        ]
+    )
+    rows = staged.shape[-1]
+    length = k_ref.shape[-1]
+    for block in range(views):
+        keys[block] = k_ref[block].T
+
+    def attend(target, half):
+        q = q_ref[target, :, pl.ds(pl.multiple_of(half * rows, rows), rows)]
+        highest = jnp.full((1, rows), -1e30, jnp.float32)
+        totals = jnp.zeros((1, rows), jnp.float32)
+        blended = jnp.zeros((HS, rows), jnp.float32)
+        for block in range(views):
+            scores = jnp.dot(keys[block], q, preferred_element_type=jnp.float32)
+            newest = jnp.maximum(highest, jnp.max(scores, 0, keepdims=True))
+            shrink = jnp.exp(highest - newest)
+            weights = jnp.exp(scores - newest)
+            totals = totals * shrink + jnp.sum(weights, 0, keepdims=True)
+            blended = blended * shrink + jnp.dot(
+                v_ref[block], weights.astype(jnp.bfloat16), preferred_element_type=jnp.float32
+            )
+            highest = newest
+        return (blended / totals).astype(jnp.bfloat16)
+
+    def copy_to(dv, dt):
+        target, half = lax.rem(view + dv, views), lax.rem(tok + dt, toks)
+        return pltpu.make_async_remote_copy(
+            src_ref=staged.at[dv, dt],
+            dst_ref=out_ref.at[tok, view],
+            send_sem=send_sem.at[dv, dt],
+            recv_sem=recv_sem.at[dv, dt],
+            device_id={"view": target, "tok": half},
+            device_id_type=MESH,
+        )
+
+    def one_view(dv, carry):
+        for dt in range(toks):
+            target, half = lax.rem(view + dv, views), lax.rem(tok + dt, toks)
+            staged[dv, dt] = attend(target, half)
+            copy_to(dv, dt).start()
+        return carry
+
+    lax.fori_loop(1, views, one_view, 0)
+    for dt in list(range(1, toks)) + [0]:
+        staged[0, dt] = attend(view, lax.rem(tok + dt, toks))
+        if dt:
+            copy_to(0, dt).start()
+    own = pltpu.make_async_copy(staged.at[0, 0], out_ref.at[tok, view], own_sem)
+    own.start()
+    for dv, dt in others:
+        copy_to(dv, dt).wait_send()
+        pltpu.make_async_remote_copy(
+            src_ref=staged.at[dv, dt],
+            dst_ref=out_ref.at[
+                lax.rem(tok - dt + toks, toks), lax.rem(view - dv + views, views)
+            ],
+            send_sem=send_sem.at[dv, dt],
+            recv_sem=recv_sem.at[dv, dt],
+            device_id={"view": view, "tok": tok},
+            device_id_type=MESH,
+        ).wait_recv()
+    own.wait()
+
+
+def attention(queries, keys, values, views, toks):
+    length = queries.shape[-1]
+    rows = length // toks
+    return pl.pallas_call(
+        functools.partial(attention_kernel, views, toks),
+        out_shape=jax.ShapeDtypeStruct((toks, views, HS, rows), jnp.bfloat16),
+        in_specs=[VMEM] * 3,
+        out_specs=ANY,
+        scratch_shapes=[
+            pltpu.VMEM((views, length, HS), jnp.bfloat16),
+            pltpu.VMEM((views, toks, HS, rows), jnp.bfloat16),
+            pltpu.SemaphoreType.DMA((views, toks)),
+            pltpu.SemaphoreType.DMA((views, toks)),
+            pltpu.SemaphoreType.DMA,
+        ],
+        compiler_params=pltpu.CompilerParams(collective_id=2, has_side_effects=True),
+        name="attention",
+    )(queries, keys, values)
+
+
+def by_heads(
+    latents,
+    query_weight,
+    key_weight,
+    value_weight,
+    output_weight,
+    value_units,
+    gate_units,
+    down_weight,
+):
+    toks, views = lax.axis_size("tok"), lax.axis_size("view")
+    head_width = query_weight.shape[1]
+    width = latents.shape[-1]
+    stream = latents.reshape(-1, width).astype(jnp.float32)
+    rows = stream.shape[0]
+    normed = normalize(stream).astype(jnp.bfloat16)
+    gathered = over_tokens(normed, toks, False, 0).reshape(toks * rows, width)
+
+    def project(weight):
+        return lax.dot_general(
+            weight, gathered, (((0,), (1,)), ((), ())), preferred_element_type=jnp.float32
+        )
+
+    def heads(projected):
+        return projected.astype(jnp.bfloat16).reshape(views, HS, toks * rows)
+
+    queries = heads(project(query_weight) * HS ** (-0.5))
+    keys, values = heads(project(key_weight)), heads(project(value_weight))
+    queries, keys, values, full_output = spread_heads(
+        queries, keys, values, output_weight, views, toks
+    )
+    attended = attention(queries, keys, values, views, toks).reshape(toks, head_width, rows)
+    group_parts = jnp.einsum(
+        "gcr,gcd->grd", attended, full_output, preferred_element_type=jnp.float32
+    ).astype(jnp.bfloat16)
+    middle = stream + jnp.sum(group_parts.astype(jnp.float32), 0)
+    normed_two = normalize(middle).astype(jnp.bfloat16)
+    gathered_two = over_tokens(normed_two, toks, False, 3).reshape(toks * rows, width)
+    linear = jnp.dot(gathered_two, value_units, preferred_element_type=jnp.float32)
+    gating = jnp.dot(gathered_two, gate_units, preferred_element_type=jnp.float32)
+    hidden = (linear * jax.nn.gelu(gating)).astype(jnp.bfloat16)
+    unit_part = jnp.dot(hidden, down_weight, preferred_element_type=jnp.float32)
+    unit_part = unit_part.astype(jnp.bfloat16).reshape(toks, rows, width)
+    parts = over_tokens(unit_part, toks, True, 4)
+    refined = middle + jnp.sum(parts.astype(jnp.float32), 0)
+    return refined.astype(jnp.bfloat16).reshape(latents.shape)
+
+
+def by_ring(
     latents,
     query_weight,
     key_weight,
@@ -125,6 +375,14 @@
     return (middle + feed_out).astype(jnp.bfloat16)
 
 
+def on_device(latents, query_weight, *weights):
+    head_count = query_weight.shape[1] // HS
+    one_each = latents.shape[1] == 1 and latents.shape[2] == 1
+    if one_each and head_count == lax.axis_size("view"):
+        return by_heads(latents, query_weight, *weights)
+    return by_ring(latents, query_weight, *weights)
+
+
 def solution(mesh):
     return jax.shard_map(
         on_device,

time: 368 us -> 194 us (0.53)
  waiting for transfers between devices: 244 us -> 0 us
  Pallas kernels: 0 us -> 152 us
  matrix products: 62 us -> 33.4 us
  other arithmetic: 25.2 us -> 8.34 us
  between operations: 13.3 us -> 0.11 us
  local copies, waits for them, and re-layouts: 11.3 us -> 0.02 us
  blocking collectives: 9.56 us -> 0 us
    ppermute x7 -> x0, waiting for transfers between devices: 174 us -> none  [passed_along(): return lax.ppermute(block, axis, route)]
    pallas_call x0 -> x5, Pallas kernels: none -> 152 us  [the longest x1 63.6 us: attention(): pl.pallas_call(functools.partial(attention_kernel, views, toks), out_shap...]
    all_gather x3 -> x0, waiting for transfers between devices: 46.5 us -> none  [the longest x1 26.3 us: on_device(): lax.all_gather(normed, 'tok', axis=0, tiled=True)]
    dot_general x20 -> x6, matrix products: 62 us -> 33.4 us  [the longest x1 14.8 us: by_heads(): unit_part = jnp.dot(hidden, down_weight, preferred_element_type=jnp.float32)]
    reduce_scatter x1 -> x0, waiting for transfers between devices: 23.4 us -> none  [on_device(): lax.psum_scatter(jnp.dot(hidden, down_weight, preferred_element_type=jnp....]
    reduce_sum x8 -> x1, other arithmetic: 14.9 us -> 1.69 us  [by_heads(): refined = middle + jnp.sum(parts.astype(jnp.float32), 0)]
    all_to_all x1 -> x0, blocking collectives: 9.56 us -> none  [on_device(): lax.all_to_all(attended, 'tok', split_axis=0, concat_axis=3, tiled=True)]
    while x15 -> x0, local copies, waits for them, and re-layouts: 8.18 us -> none
  transfers between devices with their start and end apart: 11 -> 0, of which waited for: 10 -> 0; matrix products, arithmetic and copies ran while one was open for 17% -> 0% of each run, Pallas kernels for 0% -> 0%
where the time goes in v1:
time: 194 us; the launch traced here: 193 us
  Pallas kernels  152 us (78%)
  matrix products  33.4 us (17%)
  other arithmetic  8.34 us (4%)
    pallas_call x1, Pallas kernels, attention(): pl.pallas_call(functools.partial(attention_kernel, views, toks), out_shap...  63.6 us
    pallas_call x3, Pallas kernels, over_tokens(): pl.pallas_call(functools.partial(token_kernel, count, scattered), out_sha...  50 us
    pallas_call x1, Pallas kernels, spread_heads(): pl.pallas_call(functools.partial(heads_kernel, views, toks), out_shape=(l...  37.9 us
    dot_general x1, matrix products, by_heads(): unit_part = jnp.dot(hidden, down_weight, preferred_element_type=jnp.float32)  14.8 us
    dot_general x1, matrix products, by_heads(): jnp.dot(gathered_two, gate_units, preferred_element_type=jnp.float32)  9.13 us
    dot_general x3, matrix products, project(): lax.dot_general(weight, gathered, (((0,), (1,)), ((), ())), preferred_ele...  6.57 us

profile of v1, /device:TPU:0, one launch (start us, length us, event | category | flops | bytes accessed | tf_op | source)
XLA Modules:
  0.0 193.3 jit_solution(8408777715342575341)
XLA Ops:
  0.0 0.0 copy-start
  0.0 0.0 copy-start.1
  0.0 1.4 convert_reduce_fusion.1
  1.4 1.4 fusion.15
  2.8 0.0 copy-done.1
  2.8 1.2 fusion.16.x_ref
  4.0 18.9 %over_tokens_0.1 = bf16[2,256,1280]{2,1,0:T(8,128)(2,1)} custom-call(bf16[256,1280]{1,0:T(8,128)(2,1)} %fusion.16.x_ref), custom_call_target="tpu_custom_call" | custom-call | tf_op jit(solution)/shard_map/over_tokens_0/pallas_call | solution.py:86
  22.9 0.0 copy-done
  23.0 0.0 copy-start.2
  23.0 0.0 copy-start.3
  23.0 3.2 %convolution_convert_fusion.2 = bf16[512,512]{0,1:T(8,128)(2,1)} fusion(bf16[512,1280]{1,0:T(8,128)(2,1)} %bitcast.52, bf16[1280,512]{1,0:T(8,128)(2,1)S(1)} %copy-done), kind=kOutput, calls=%fused_computation.29 | convolution fusion | flops 671350784 | bytes 3145728 | tf_op jit(solution)/shard_map/dot_general | solution.py:246
  26.2 0.0 copy-done.2
  26.2 0.0 copy-done.3
  26.2 0.0 copy-start.4
  26.2 1.7 convolution_convert_fusion.3
  27.9 0.0 copy-done.4
  27.9 1.7 fusion.19
  29.6 37.9 %spread_heads.1 = (bf16[8,64,512]{2,1,0:T(8,128)(2,1)}, bf16[8,64,512]{2,1,0:T(8,128)(2,1)}, bf16[8,64,512]{2,1,0:T(8,128)(2,1)}, bf16[2,512,1280]{2,1,0:T(8,128)(2,1)}) custom-call(bf16[8,64,512]{2,1,0:T(8,128)(2,1)} %bitcast.59, bf16[8,64,512]{2,1,0:T(8,128)(2,1)} %bitcast.58, bf16[8,64,512]{2,1,0:T(8,128)(2,1)} %bitcast.57, bf16[512,1280]{1,0:T(8,128)(2,1)} %w.1), custom_call_target="tpu_custom_call" | custom-call | tf_op jit(solution)/shard_map/spread_heads/pallas_call | solution.py:114
  67.5 63.6 %attention.1 = bf16[2,8,64,256]{3,2,1,0:T(8,128)(2,1)} custom-call(bf16[8,64,512]{2,1,0:T(8,128)(2,1)} %get-tuple-element.9.q_ref, bf16[8,64,512]{2,1,0:T(8,128)(2,1)} %get-tuple-element.10.k_ref, bf16[8,64,512]{2,1,0:T(8,128)(2,1)} %get-tuple-element.11.v_ref), custom_call_target="tpu_custom_call" | custom-call | tf_op jit(solution)/shard_map/attention/pallas_call | solution.py:210
  131.1 2.9 %fusion.12 = f32[256,1280]{1,0:T(8,128)S(1)} fusion(bf16[2,512,256]{2,1,0:T(8,128)(2,1)} %bitcast.50, bf16[2,512,1280]{2,1,0:T(8,128)(2,1)} %get-tuple-element.12), kind=kOutput, calls=%fused_computation.19 | convolution fusion | flops 672727040 | bytes 4456448 | tf_op jit(solution)/shard_map/gcr,gcd->grd/dot_general | solution.py:259
  134.0 0.2 fusion.20
  134.2 0.3 multiply_reduce_fusion
  134.5 1.1 multiply_convert_fusion.x_ref
  135.6 15.9 %over_tokens_3.1 = bf16[2,256,1280]{2,1,0:T(8,128)(2,1)} custom-call(bf16[256,1280]{1,0:T(8,128)(2,1)} %multiply_convert_fusion.x_ref), custom_call_target="tpu_custom_call" | custom-call | tf_op jit(solution)/shard_map/over_tokens_3/pallas_call | solution.py:86
  151.5 9.1 %fusion.25 = f32[512,2560]{1,0:T(8,128)} fusion(bf16[512,1280]{1,0:T(8,128)(2,1)} %bitcast.55, bf16[1280,2560]{1,0:T(8,128)(2,1)} %param.14), kind=kOutput, calls=%fused_computation.41 | convolution fusion | flops 3355443200 | bytes 13107200 | tf_op jit(solution)/shard_map/dot_general | solution.py:266
  160.6 14.8 %convolution_convert_fusion = bf16[512,1280]{1,0:T(8,128)(2,1)} fusion(bf16[2560,1280]{1,0:T(8,128)(2,1)} %param.15, f32[512,2560]{1,0:T(8,128)} %fusion.25, bf16[512,1280]{1,0:T(8,128)(2,1)} %bitcast.56, bf16[1280,2560]{1,0:T(8,128)(2,1)} %param.13), kind=kOutput, calls=%fused_computation.10 | convolution fusion | flops 6724648960 | bytes 20971520 | tf_op jit(solution)/shard_map/dot_general | solution.py:268
  175.4 15.2 %over_tokens_4.1 = bf16[2,256,1280]{2,1,0:T(8,128)(2,1)} custom-call(bf16[2,256,1280]{2,1,0:T(8,128)(2,1)} %bitcast.51), custom_call_target="tpu_custom_call" | custom-call | tf_op jit(solution)/shard_map/over_tokens_4/pallas_call | solution.py:86
  190.6 1.7 convert_reduce_fusion
  192.3 1.1 fusion.18
  (4 shorter events, 0.0 us)
Async XLA Ops:
  0.0 22.9 %copy-start = (bf16[1280,512]{1,0:T(8,128)(2,1)S(1)}, bf16[1280,512]{1,0:T(8,128)(2,1)}, u32[]{:S(2)}) copy-start(bf16[1280,512]{1,0:T(8,128)(2,1)} %param.11) | copy-start | bytes 3932164
  0.0 2.8 %copy-start.1 = (bf16[256,1,1,1280]{3,0,2,1:T(8,128)(2,1)S(1)}, bf16[256,1,1,1280]{3,0,2,1:T(8,128)(2,1)}, u32[]{:S(2)}) copy-start(bf16[256,1,1,1280]{3,0,2,1:T(8,128)(2,1)} %param.8) | copy-start | bytes 1966084
  23.0 3.2 %copy-start.2 = (bf16[2,256,1280]{2,1,0:T(8,128)(2,1)S(1)}, bf16[2,256,1280]{2,1,0:T(8,128)(2,1)}, u32[]{:S(2)}) copy-start(bf16[2,256,1280]{2,1,0:T(8,128)(2,1)} %over_tokens_0.1) | copy-start | bytes 3932164
  23.0 3.2 %copy-start.3 = (bf16[1280,512]{1,0:T(8,128)(2,1)S(1)}, bf16[1280,512]{1,0:T(8,128)(2,1)}, u32[]{:S(2)}) copy-start(bf16[1280,512]{1,0:T(8,128)(2,1)} %param.10) | copy-start | bytes 3932164
  26.2 1.7 copy-start.4

commit v2 on v1

--- a/solution.py
+++ b/solution.py
@@ -130,7 +130,7 @@
 
 
 def attention_kernel(
-    views, toks, q_ref, k_ref, v_ref, out_ref, keys, staged, send_sem, recv_sem, own_sem
+    views, toks, q_ref, k_ref, v_ref, out_ref, keys, scores, staged, send_sem, recv_sem, own_sem
 ):
     view, tok = lax.axis_index("view"), lax.axis_index("tok")
     others = [
@@ -147,27 +147,32 @@
     for block in range(views):
         keys[block] = k_ref[block].T
 
-    def attend(target, half):
-        q = q_ref[target, :, pl.ds(pl.multiple_of(half * rows, rows), rows)]
-        highest = jnp.full((1, rows), -1e30, jnp.float32)
-        totals = jnp.zeros((1, rows), jnp.float32)
-        blended = jnp.zeros((HS, rows), jnp.float32)
+    def attend(target):
+        q = q_ref[target]
+        highest = jnp.full((1, length), -1e30, jnp.float32)
         for block in range(views):
-            scores = jnp.dot(keys[block], q, preferred_element_type=jnp.float32)
-            newest = jnp.maximum(highest, jnp.max(scores, 0, keepdims=True))
-            shrink = jnp.exp(highest - newest)
-            weights = jnp.exp(scores - newest)
-            totals = totals * shrink + jnp.sum(weights, 0, keepdims=True)
-            blended = blended * shrink + jnp.dot(
+            found = jnp.dot(keys[block], q, preferred_element_type=jnp.float32)
+            scores[block] = found
+            highest = jnp.maximum(highest, jnp.max(found, 0, keepdims=True))
+        totals = jnp.zeros((1, length), jnp.float32)
+        blended = jnp.zeros((HS, length), jnp.float32)
+        for block in range(views):
+            weights = jnp.exp(scores[block] - highest)
+            totals = totals + jnp.sum(weights, 0, keepdims=True)
+            blended = blended + jnp.dot(
                 v_ref[block], weights.astype(jnp.bfloat16), preferred_element_type=jnp.float32
             )
-            highest = newest
         return (blended / totals).astype(jnp.bfloat16)
+
+    def stage(dv):
+        attended = attend(lax.rem(view + dv, views))
+        for half in range(toks):
+            staged[dv, half] = attended[:, half * rows : (half + 1) * rows]
 
     def copy_to(dv, dt):
         target, half = lax.rem(view + dv, views), lax.rem(tok + dt, toks)
         return pltpu.make_async_remote_copy(
-            src_ref=staged.at[dv, dt],
+            src_ref=staged.at[dv, half],
             dst_ref=out_ref.at[tok, view],
             send_sem=send_sem.at[dv, dt],
             recv_sem=recv_sem.at[dv, dt],
@@ -176,18 +181,16 @@
         )
 
     def one_view(dv, carry):
+        stage(dv)
         for dt in range(toks):
-            target, half = lax.rem(view + dv, views), lax.rem(tok + dt, toks)
-            staged[dv, dt] = attend(target, half)
             copy_to(dv, dt).start()
         return carry
 
     lax.fori_loop(1, views, one_view, 0)
-    for dt in list(range(1, toks)) + [0]:
-        staged[0, dt] = attend(view, lax.rem(tok + dt, toks))
-        if dt:
-            copy_to(0, dt).start()
-    own = pltpu.make_async_copy(staged.at[0, 0], out_ref.at[tok, view], own_sem)
+    stage(0)
+    for dt in range(1, toks):
+        copy_to(0, dt).start()
+    own = pltpu.make_async_copy(staged.at[0, tok], out_ref.at[tok, view], own_sem)
     own.start()
     for dv, dt in others:
         copy_to(dv, dt).wait_send()
@@ -214,6 +217,7 @@
         out_specs=ANY,
         scratch_shapes=[
             pltpu.VMEM((views, length, HS), jnp.bfloat16),
+            pltpu.VMEM((views, length, length), jnp.float32),
             pltpu.VMEM((views, toks, HS, rows), jnp.bfloat16),
             pltpu.SemaphoreType.DMA((views, toks)),
             pltpu.SemaphoreType.DMA((views, toks)),
@@ -261,15 +265,22 @@
     ).astype(jnp.bfloat16)
     middle = stream + jnp.sum(group_parts.astype(jnp.float32), 0)
     normed_two = normalize(middle).astype(jnp.bfloat16)
-    gathered_two = over_tokens(normed_two, toks, False, 3).reshape(toks * rows, width)
-    linear = jnp.dot(gathered_two, value_units, preferred_element_type=jnp.float32)
-    gating = jnp.dot(gathered_two, gate_units, preferred_element_type=jnp.float32)
-    hidden = (linear * jax.nn.gelu(gating)).astype(jnp.bfloat16)
-    unit_part = jnp.dot(hidden, down_weight, preferred_element_type=jnp.float32)
-    unit_part = unit_part.astype(jnp.bfloat16).reshape(toks, rows, width)
-    parts = over_tokens(unit_part, toks, True, 4)
-    refined = middle + jnp.sum(parts.astype(jnp.float32), 0)
-    return refined.astype(jnp.bfloat16).reshape(latents.shape)
+
+    def feed(block):
+        linear = jnp.dot(block, value_units, preferred_element_type=jnp.float32)
+        gating = jnp.dot(block, gate_units, preferred_element_type=jnp.float32)
+        hidden = (linear * jax.nn.gelu(gating)).astype(jnp.bfloat16)
+        return jnp.dot(hidden, down_weight, preferred_element_type=jnp.float32).astype(jnp.bfloat16)
+
+    pieces = jnp.split(normed_two, 2 if rows % 32 == 0 else 1)
+    arrived = [
+        [passed_along(piece, "tok", d) for piece in pieces] for d in range(1, toks)
+    ]
+    total = middle + lax.optimization_barrier(feed(normed_two)).astype(jnp.float32)
+    for d, blocks in enumerate(arrived, 1):
+        back = [passed_along(feed(block), "tok", -d) for block in blocks]
+        total = total + jnp.concatenate(back, 0).astype(jnp.float32)
+    return total.astype(jnp.bfloat16).reshape(latents.shape)
 
 
 def by_ring(

time: 194 us -> 157 us (0.81)
  Pallas kernels: 152 us -> 91.4 us
  matrix products: 33.4 us -> 47.3 us
  waiting for transfers between devices: 0 us -> 5.19 us
  starting transfers between devices: 0 us -> 4.05 us
    pallas_call x3 -> x1, Pallas kernels: 50 us -> 18.9 us  [over_tokens(): pl.pallas_call(functools.partial(token_kernel, count, scattered), out_sha...]
    pallas_call x1, Pallas kernels: 63.6 us -> 34.5 us  [attention(): pl.pallas_call(functools.partial(attention_kernel, views, toks), out_shap...]
    dot_general x2 -> x6, matrix products: 23.9 us -> 37.7 us  [the longest x3 27.1 us: feed(): jnp.dot(hidden, down_weight, preferred_element_type=jnp.float32)]
    ppermute x0 -> x4, waiting for transfers between devices: none -> 5.19 us  [passed_along(): return lax.ppermute(block, axis, route)]
    ppermute x0 -> x4, starting transfers between devices: none -> 4.05 us  [passed_along(): return lax.ppermute(block, axis, route)]
    reshape x0 -> x1, other arithmetic: none -> 2.38 us  [by_heads(): return total.astype(jnp.bfloat16).reshape(latents.shape)]
  transfers between devices with their start and end apart: 0 -> 4, of which waited for: 0 -> 1; matrix products, arithmetic and copies ran while one was open for 0% -> 24% of each run, Pallas kernels for 0% -> 0%
where the time goes in v2:
time: 157 us
  Pallas kernels  91.4 us (58%)
  matrix products  47.3 us (30%)
  other arithmetic  7.14 us (5%)
  waiting for transfers between devices  5.19 us (3%)
  starting transfers between devices  4.05 us (3%)
  local copies, waits for them, and re-layouts  1.6 us (1%)
    pallas_call x1, Pallas kernels, spread_heads(): pl.pallas_call(functools.partial(heads_kernel, views, toks), out_shape=(l...  37.9 us
    pallas_call x1, Pallas kernels, attention(): pl.pallas_call(functools.partial(attention_kernel, views, toks), out_shap...  34.5 us
    dot_general x3, matrix products, feed(): jnp.dot(hidden, down_weight, preferred_element_type=jnp.float32)  27.1 us
    pallas_call x1, Pallas kernels, over_tokens(): pl.pallas_call(functools.partial(token_kernel, count, scattered), out_sha...  18.9 us
    dot_general x3, matrix products, feed(): gating = jnp.dot(block, gate_units, preferred_element_type=jnp.float32)  10.5 us
    dot_general x3, matrix products, project(): lax.dot_general(weight, gathered, (((0,), (1,)), ((), ())), preferred_ele...  6.55 us
    ppermute x4, waiting for transfers between devices, passed_along(): return lax.ppermute(block, axis, route)  5.19 us
    ppermute x4, starting transfers between devices, passed_along(): return lax.ppermute(block, axis, route)  4.05 us
  transfers between devices with their start and end apart: 4, of which 1 were waited for; matrix products, arithmetic and copies ran while one was open for 24% of the time, Pallas kernels for 0%

profile of v2, /device:TPU:0, one launch (start us, length us, event | category | flops | bytes accessed | tf_op | source)
XLA Modules:
  0.0 156.7 jit_solution(13076310862860998566)
XLA Ops:
  0.0 0.0 copy-start
  0.0 0.0 copy-start.1
  0.0 1.4 convert_reduce_fusion
  1.4 1.4 fusion.16
  2.8 0.0 copy-done.1
  2.8 1.2 fusion.17.x_ref
  4.0 18.9 %over_tokens_0.1 = bf16[2,256,1280]{2,1,0:T(8,128)(2,1)} custom-call(bf16[256,1280]{1,0:T(8,128)(2,1)} %fusion.17.x_ref), custom_call_target="tpu_custom_call" | custom-call | tf_op jit(solution)/shard_map/over_tokens_0/pallas_call | solution.py:86
  22.9 0.0 copy-done
  23.0 0.0 copy-start.3
  23.0 0.0 copy-start.5
  23.0 3.2 %fusion.32 = bf16[512,512]{0,1:T(8,128)(2,1)} fusion(bf16[512,1280]{1,0:T(8,128)(2,1)} %bitcast.61, bf16[1280,512]{1,0:T(8,128)(2,1)S(1)} %copy-done), kind=kOutput, calls=%fused_computation.50 | convolution fusion | flops 671612928 | bytes 3145728 | tf_op jit(solution)/shard_map/dot_general | solution.py:250
  26.1 0.0 copy-done.3
  26.1 0.0 copy-done.5
  26.1 0.0 copy-start.6
  26.1 1.7 %convolution_convert_fusion.5 = bf16[512,512]{0,1:T(8,128)(2,1)} fusion(bf16[512,1280]{1,0:T(8,128)(2,1)S(1)} %bitcast.62, bf16[1280,512]{1,0:T(8,128)(2,1)S(1)} %copy-done.5), kind=kOutput, calls=%fused_computation.49 | convolution fusion | flops 671350784 | bytes 3145728 | tf_op jit(solution)/shard_map/dot_general | solution.py:250
  27.8 0.0 copy-done.6
  27.8 1.7 %convolution_convert_fusion.4 = bf16[512,512]{0,1:T(8,128)(2,1)} fusion(bf16[512,1280]{1,0:T(8,128)(2,1)S(1)} %bitcast.63, bf16[1280,512]{1,0:T(8,128)(2,1)S(1)} %copy-done.6), kind=kOutput, calls=%fused_computation.48 | convolution fusion | flops 671350784 | bytes 3145728 | tf_op jit(solution)/shard_map/dot_general | solution.py:250
  29.5 37.9 %spread_heads.1 = (bf16[8,64,512]{2,1,0:T(8,128)(2,1)}, bf16[8,64,512]{2,1,0:T(8,128)(2,1)}, bf16[8,64,512]{2,1,0:T(8,128)(2,1)}, bf16[2,512,1280]{2,1,0:T(8,128)(2,1)}) custom-call(bf16[8,64,512]{2,1,0:T(8,128)(2,1)} %bitcast.64, bf16[8,64,512]{2,1,0:T(8,128)(2,1)} %bitcast.65, bf16[8,64,512]{2,1,0:T(8,128)(2,1)} %bitcast.66, bf16[512,1280]{1,0:T(8,128)(2,1)} %w.1), custom_call_target="tpu_custom_call" | custom-call | tf_op jit(solution)/shard_map/spread_heads/pallas_call | solution.py:114
  67.5 34.5 %attention.1 = bf16[2,8,64,256]{3,2,1,0:T(8,128)(2,1)} custom-call(bf16[8,64,512]{2,1,0:T(8,128)(2,1)} %get-tuple-element.9.q_ref, bf16[8,64,512]{2,1,0:T(8,128)(2,1)} %get-tuple-element.10.k_ref, bf16[8,64,512]{2,1,0:T(8,128)(2,1)} %get-tuple-element.11.v_ref), custom_call_target="tpu_custom_call" | custom-call | tf_op jit(solution)/shard_map/attention/pallas_call | solution.py:213
  102.0 0.0 slice-start
  102.0 3.0 %fusion.13 = f32[256,1280]{1,0:T(8,128)S(1)} fusion(bf16[2,512,256]{2,1,0:T(8,128)(2,1)} %bitcast.60, bf16[2,512,1280]{2,1,0:T(8,128)(2,1)} %get-tuple-element.12), kind=kOutput, calls=%fused_computation.25 | convolution fusion | flops 672727040 | bytes 4456448 | tf_op jit(solution)/shard_map/gcr,gcd->grd/dot_general | solution.py:263
  105.0 0.0 slice-start.1
  105.0 0.2 fusion.34
  105.3 0.3 multiply_reduce_fusion
  105.6 0.2 multiply_convert_fusion
  105.8 0.0 copy-start.2
  105.8 0.8 fusion.47
  106.7 1.5 collective-permute-start.2
  108.2 0.6 collective-permute-start
  108.7 0.0 slice-done
  108.7 0.0 slice-done.1
  108.7 3.4 %fusion.48 = f32[256,2560]{1,0:T(8,128)} fusion(bf16[256,1280]{1,0:T(8,128)(2,1)S(1)} %multiply_convert_fusion, bf16[1280,2560]{1,0:T(8,128)(2,1)S(1)} %bitcast.59), kind=kOutput, calls=%fused_computation.70 | convolution fusion | flops 1677721600 | bytes 9830400 | tf_op jit(solution)/shard_map/dot_general | solution.py:271
  112.1 0.0 copy-done.2
  112.1 5.2 %collective-permute-done.2 = bf16[128,1280]{1,0:T(8,128)(2,1)S(1)} collective-permute-done((bf16[128,1280]{1,0:T(8,128)(2,1)S(1)}, bf16[128,1280]{1,0:T(8,128)(2,1)S(1)}, u32[]{:S(2)}, u32[]{:S(2)}) %collective-permute-start.2) | collective-permute-done | bytes 327712 | tf_op jit(solution)/shard_map/ppermute | solution.py:22
  117.3 0.0 copy-start.4
  117.3 0.7 copy-done.4
  118.0 2.1 %fusion.50 = f32[128,2560]{1,0:T(8,128)} fusion(bf16[128,1280]{1,0:T(8,128)(2,1)S(1)} %collective-permute-done.2, bf16[1280,2560]{1,0:T(8,128)(2,1)S(1)} %bitcast.59), kind=kOutput, calls=%fused_computation.72 | convolution fusion | flops 838860800 | bytes 8192000 | tf_op jit(solution)/shard_map/dot_general | solution.py:271
  120.1 8.3 %convolution_convert_fusion.2 = bf16[128,1280]{1,0:T(8,128)(2,1)} fusion(bf16[2560,1280]{1,0:T(8,128)(2,1)} %param.15, bf16[128,1280]{1,0:T(8,128)(2,1)} %copy-done.4, bf16[1280,2560]{1,0:T(8,128)(2,1)} %param.13, f32[128,2560]{1,0:T(8,128)} %fusion.50), kind=kOutput, calls=%fused_computation.17 | convolution fusion | flops 1681162240 | bytes 15073280 | tf_op jit(solution)/shard_map/dot_general | solution.py:273
  128.4 1.5 collective-permute-start.3
  129.9 0.0 collective-permute-done
  129.9 5.1 %fusion.49 = f32[128,2560]{1,0:T(8,128)} fusion(bf16[128,1280]{1,0:T(8,128)(2,1)} %collective-permute-done, bf16[1280,2560]{1,0:T(8,128)(2,1)} %param.14), kind=kOutput, calls=%fused_computation.71 | convolution fusion | flops 838860800 | bytes 8192000 | tf_op jit(solution)/shard_map/dot_general | solution.py:271
  135.0 8.3 %convolution_convert_fusion.3 = bf16[128,1280]{1,0:T(8,128)(2,1)} fusion(bf16[2560,1280]{1,0:T(8,128)(2,1)} %param.15, bf16[128,1280]{1,0:T(8,128)(2,1)} %collective-permute-done, bf16[1280,2560]{1,0:T(8,128)(2,1)} %param.13, f32[128,2560]{1,0:T(8,128)} %fusion.49), kind=kOutput, calls=%fused_computation.18 | convolution fusion | flops 1681162240 | bytes 15073280 | tf_op jit(solution)/shard_map/dot_general | solution.py:273
  143.3 0.6 collective-permute-start.1
  143.9 10.5 %convolution_convert_fusion.1 = bf16[256,1280]{1,0:T(8,128)(2,1)} fusion(bf16[2560,1280]{1,0:T(8,128)(2,1)} %param.15, bf16[256,1280]{1,0:T(8,128)(2,1)} %copy-done.2, bf16[1280,2560]{1,0:T(8,128)(2,1)} %param.13, f32[256,2560]{1,0:T(8,128)} %fusion.48), kind=kOutput, calls=%fused_computation.16 | convolution fusion | flops 3362324480 | bytes 17039360 | tf_op jit(solution)/shard_map/dot_general | solution.py:273
  154.3 0.0 collective-permute-done.3
  154.3 0.0 collective-permute-done.1
  154.3 2.4 %fusion.33 = bf16[256,1,1,1280]{3,0,2,1:T(8,128)(2,1)} fusion(bf16[256,1280]{1,0:T(8,128)(2,1)} %convolution_convert_fusion.1, bf16[128,1280]{1,0:T(8,128)(2,1)} %collective-permute-done.3, bf16[128,1280]{1,0:T(8,128)(2,1)} %collective-permute-done.1, f32[256,1280]{1,0:T(8,128)S(1)} %fusion.13, bf16[256,1,1,1280]{3,0,2,1:T(8,128)(2,1)S(1)} %copy-done.1), kind=kLoop, calls=%fused_computation.51 | loop fusion | flops 3276800 | bytes 3932160 | tf_op jit(solution)/shard_map/reshape | solution.py:283
  (5 shorter events, 0.0 us)
Async XLA Ops:
  0.0 22.9 %copy-start = (bf16[1280,512]{1,0:T(8,128)(2,1)S(1)}, bf16[1280,512]{1,0:T(8,128)(2,1)}, u32[]{:S(2)}) copy-start(bf16[1280,512]{1,0:T(8,128)(2,1)} %param.9) | copy-start | bytes 3932164
  0.0 2.8 %copy-start.1 = (bf16[256,1,1,1280]{3,0,2,1:T(8,128)(2,1)S(1)}, bf16[256,1,1,1280]{3,0,2,1:T(8,128)(2,1)}, u32[]{:S(2)}) copy-start(bf16[256,1,1,1280]{3,0,2,1:T(8,128)(2,1)} %param.8) | copy-start | bytes 1966084
  23.0 3.2 %copy-start.3 = (bf16[2,256,1280]{2,1,0:T(8,128)(2,1)S(1)}, bf16[2,256,1280]{2,1,0:T(8,128)(2,1)}, u32[]{:S(2)}) copy-start(bf16[2,256,1280]{2,1,0:T(8,128)(2,1)} %over_tokens_0.1) | copy-start | bytes 3932164
  23.0 3.2 %copy-start.5 = (bf16[1280,512]{1,0:T(8,128)(2,1)S(1)}, bf16[1280,512]{1,0:T(8,128)(2,1)}, u32[]{:S(2)}) copy-start(bf16[1280,512]{1,0:T(8,128)(2,1)} %param.10) | copy-start | bytes 3932164
  26.1 1.7 %copy-start.6 = (bf16[1280,512]{1,0:T(8,128)(2,1)S(1)}, bf16[1280,512]{1,0:T(8,128)(2,1)}, u32[]{:S(2)}) copy-start(bf16[1280,512]{1,0:T(8,128)(2,1)} %param.11) | copy-start | bytes 3932164
  102.0 6.7 %slice-start = ((s8[6553600]{0:T(1024)(128)(4,1)}), s8[4194304]{0:T(1024)(128)(4,1)S(1)}, s32[]{:S(2)}) async-start(s8[6553600]{0:T(1024)(128)(4,1)} %bitcast.58), calls=%async_computation | async-start | bytes 8388608
  105.0 3.7 %slice-start.1 = ((s8[6553600]{0:T(1024)(128)(4,1)}), s8[2359296]{0:T(1024)(128)(4,1)S(1)}, s32[]{:S(2)}) async-start(s8[6553600]{0:T(1024)(128)(4,1)} %bitcast.58), calls=%async_computation.1 | async-start | bytes 4718592
  105.8 6.3 %copy-start.2 = (bf16[256,1280]{1,0:T(8,128)(2,1)}, bf16[256,1280]{1,0:T(8,128)(2,1)S(1)}, u32[]{:S(2)}) copy-start(bf16[256,1280]{1,0:T(8,128)(2,1)S(1)} %multiply_convert_fusion) | copy-start | bytes 1966084
  106.7 10.6 %collective-permute-start.2 = (bf16[128,1280]{1,0:T(8,128)(2,1)S(1)}, bf16[128,1280]{1,0:T(8,128)(2,1)S(1)}, u32[]{:S(2)}, u32[]{:S(2)}) collective-permute-start(bf16[128,1280]{1,0:T(8,128)(2,1)S(1)} %get-tuple-element.14), channel_id=1, source_target_pairs={{2,0},{0,2},{3,1},{1,3},{6,4},{4,6},{7,5},{5,7},{10,8},{8,10},{11,... | collective-permute-start | bytes 983048 | tf_op jit(solution)/shard_map/ppermute | solution.py:22
  108.2 21.7 %collective-permute-start = (bf16[128,1280]{1,0:T(8,128)(2,1)}, bf16[128,1280]{1,0:T(8,128)(2,1)}, u32[]{:S(2)}, u32[]{:S(2)}) collective-permute-start(bf16[128,1280]{1,0:T(8,128)(2,1)} %get-tuple-element.13), channel_id=1, source_target_pairs={{2,0},{0,2},{3,1},{1,3},{6,4},{4,6},{7,5},{5,7},{10,8},{8,10},{11,... | collective-permute-start | bytes 983048 | tf_op jit(solution)/shard_map/ppermute | solution.py:22
  117.3 0.7 copy-start.4
  128.4 25.9 %collective-permute-start.3 = (bf16[128,1280]{1,0:T(8,128)(2,1)}, bf16[128,1280]{1,0:T(8,128)(2,1)}, u32[]{:S(2)}, u32[]{:S(2)}) collective-permute-start(bf16[128,1280]{1,0:T(8,128)(2,1)} %convolution_convert_fusion.2), channel_id=1, source_target_pairs={{2,0},{0,2},{3,1},{1,3},{6,4},{4,6},{7,5},{5,7},{10,8},{8,10},{11,... | collective-permute-start | bytes 983048 | tf_op jit(solution)/shard_map/ppermute | solution.py:22
  143.3 11.0 %collective-permute-start.1 = (bf16[128,1280]{1,0:T(8,128)(2,1)}, bf16[128,1280]{1,0:T(8,128)(2,1)}, u32[]{:S(2)}, u32[]{:S(2)}) collective-permute-start(bf16[128,1280]{1,0:T(8,128)(2,1)} %convolution_convert_fusion.3), channel_id=1, source_target_pairs={{2,0},{0,2},{3,1},{1,3},{6,4},{4,6},{7,5},{5,7},{10,8},{8,10},{11,... | collective-permute-start | bytes 983048 | tf_op jit(solution)/shard_map/ppermute | solution.py:22
